TPU v7x, 32 devices: a whole 2x2x4 slice. The times are simulated.
32 devices in a mesh: grp: 2 (over y), wide: 8 (over z, x), narrow: 2 (over core).
Axes of the slice: x: 2, y: 2, z: 4, core: 2. Of those that a mesh axis runs over, the one named last changes fastest.
Arguments:
- cache: bfloat16 [16, 48, 576], P('grp', ('wide', 'narrow')), parts along dimension 0, may hold values from -4 to 4
- lengths: int32 [16], P('grp'), parts along dimension 0, may hold values from 1 to 47, 128 in all
- slots: int32 [16], P('grp'), parts along dimension 0, may hold values from 0 to 7, each once
- query: bfloat16 [16, 1, 64, 576], P(('grp', 'wide'), None, 'narrow'), parts along dimension 0, may hold values from -200 to 200
Outputs:
- attended: bfloat16 [16, 1, 64, 512], P(('grp', 'wide'), None, 'narrow'), parts along dimension 0
There are 2 independent parts, one for each index of `grp`. A program takes and returns all parts, laid end to end along the dimension named above; each array names one. Nothing has to cross between parts.
Inputs may be any that keep to these rules, and one draw needn't show every extreme that they name: `lengths`: each request has at most 47 cached positions, and some request has exactly that many in every draw; its 1 new tokens' entries follow its cached positions. `slots`: A permutation: every slot holds one request.
All inputs are finite; a program needn't handle non-finite values.
Results may differ from a plain program's by a relative error of at most 0.013.
Values may be sent and summed in bfloat16 or wider, within the bound.
A program may use at most 64 MiB of HBM per device.

v0:
```python
import functools

import jax
import jax.numpy as jnp
from jax import lax
from jax.experimental import pallas as pl
from jax.experimental.pallas import tpu as pltpu
from jax.sharding import PartitionSpec as P

LATENT_WIDTH = 512
UNROLL_LIMIT = 16

score_scale = 0.0721687836
floor_value = -1e30


def loop(count, body):
    if count <= UNROLL_LIMIT:
        for step in range(count):
            body(step)
    else:
        lax.fori_loop(0, count, lambda step, carry: (body(step), carry)[1], 0)


def kernel(
    wide_count,
    narrow_count,
    cache_hbm,
    lengths_hbm,
    slots_hbm,
    query_hbm,
    out_ref,
    cache_ref,
    lengths_ref,
    slots_ref,
    query_ref,
    outgoing,
    received,
    local_sem,
    send_sem,
    recv_sem,
):
    wide_index = lax.axis_index("wide")
    narrow_index = lax.axis_index("narrow")
    me = wide_index * narrow_count + narrow_index
    peer_count = wide_count * narrow_count
    shard_rows, request_count, channels = cache_ref.shape
    slab_rows = outgoing.shape[1]

    slots_copy = pltpu.make_async_copy(slots_hbm, slots_ref, local_sem.at[0])
    cache_copy = pltpu.make_async_copy(cache_hbm, cache_ref, local_sem.at[1])
    lengths_copy = pltpu.make_async_copy(lengths_hbm, lengths_ref, local_sem.at[2])
    query_copy = pltpu.make_async_copy(query_hbm, query_ref, local_sem.at[3])
    slots_copy.start()
    cache_copy.start()
    lengths_copy.start()
    query_copy.start()

    def peer(step):
        target = lax.rem(me + step + 1, peer_count)
        return lax.div(target, narrow_count), lax.rem(target, narrow_count)

    barrier = pltpu.get_barrier_semaphore()

    def greet(step):
        wide_peer, narrow_peer = peer(step)
        pl.semaphore_signal(
            barrier,
            inc=1,
            device_id={"wide": wide_peer, "narrow": narrow_peer},
            device_id_type=pl.DeviceIdType.MESH,
        )

    loop(peer_count - 1, greet)
    slots_copy.wait()
    cache_copy.wait()

    slot_row = slots_ref[...].reshape(1, request_count)
    shape = (request_count * slab_rows, request_count)
    row = lax.broadcasted_iota(jnp.int32, shape, 0)
    ordered = None
    for offset in range(shard_rows):
        pick = (slot_row * slab_rows + offset == row).astype(jnp.float32).astype(jnp.bfloat16)
        term = jnp.dot(pick, cache_ref[offset], preferred_element_type=jnp.float32)
        ordered = term if ordered is None else ordered + term
    outgoing[...] = ordered.reshape(outgoing.shape).astype(jnp.bfloat16)
    received[me] = outgoing[wide_index]
    pl.semaphore_wait(barrier, peer_count - 1)

    def send(step):
        wide_peer, narrow_peer = peer(step)
        pltpu.make_async_remote_copy(
            src_ref=outgoing.at[wide_peer],
            dst_ref=received.at[me],
            send_sem=send_sem,
            recv_sem=recv_sem,
            device_id={"wide": wide_peer, "narrow": narrow_peer},
            device_id_type=pl.DeviceIdType.MESH,
        ).start()

    loop(peer_count - 1, send)
    lengths_copy.wait()
    query_copy.wait()
    own_length = jnp.sum(
        jnp.where(
            slot_row == wide_index,
            lengths_ref[...].reshape(1, request_count).astype(jnp.float32),
            0.0,
        ),
        axis=1,
        keepdims=True,
    )
    _, forward_steps, head_count, _ = query_ref.shape
    score_shape = (forward_steps * head_count, peer_count * slab_rows)
    query_rows = query_ref[...].reshape(score_shape[0], channels)
    column = lax.broadcasted_iota(jnp.int32, score_shape, 1)
    offset = column % slab_rows
    place = column // slab_rows * shard_rows + offset
    token = lax.broadcasted_iota(jnp.int32, score_shape, 0) // head_count
    visible = (offset < shard_rows) & ((place - token).astype(jnp.float32) < own_length + 1.0)
    whole = received.at[pl.ds(0, peer_count - 1)]
    pltpu.make_async_copy(whole, whole, recv_sem).wait()

    keys = received[...].reshape(peer_count * slab_rows, channels)
    scores = (
        lax.dot_general(
            query_rows, keys, (((1,), (1,)), ((), ())), preferred_element_type=jnp.float32
        )
        * score_scale
    )
    scores = jnp.where(visible, scores, floor_value)
    highest = jnp.max(scores, axis=1, keepdims=True)
    weights = jnp.where(visible, jnp.exp(scores - highest), 0.0)
    weight_sum = jnp.sum(weights, axis=1, keepdims=True)
    latent_total = jnp.dot(
        weights.astype(jnp.bfloat16), keys[:, :LATENT_WIDTH], preferred_element_type=jnp.float32
    )
    out_ref[...] = (latent_total / weight_sum).astype(jnp.bfloat16).reshape(out_ref.shape)
    pltpu.make_async_copy(whole, whole, send_sem).wait()


def padded_bytes(rows, columns):
    return rows * -(-columns // 128) * 128 * 4


def shards(cache, lengths, slots, query):
    wide_count = lax.axis_size("wide")
    narrow_count = lax.axis_size("narrow")
    peer_count = wide_count * narrow_count
    request_count, shard_rows, channels = cache.shape
    _, forward_steps, head_count, _ = query.shape
    slab_rows = pl.next_power_of_2(shard_rows)
    slabs = (request_count + peer_count) * slab_rows
    limit = (4 << 20) + 4 * padded_bytes(slabs, channels)
    return pl.pallas_call(
        functools.partial(kernel, wide_count, narrow_count),
        out_shape=jax.ShapeDtypeStruct((1, forward_steps, head_count, LATENT_WIDTH), jnp.bfloat16),
        in_specs=[pl.BlockSpec(memory_space=pltpu.HBM)] * 4,
        out_specs=pl.BlockSpec(memory_space=pltpu.VMEM),
        scratch_shapes=[
            pltpu.VMEM((shard_rows, request_count, channels), cache.dtype),
            pltpu.VMEM(lengths.shape, lengths.dtype),
            pltpu.VMEM(slots.shape, slots.dtype),
            pltpu.VMEM(query.shape, query.dtype),
            pltpu.VMEM((request_count, slab_rows, channels), cache.dtype),
            pltpu.VMEM((peer_count, slab_rows, channels), cache.dtype),
            pltpu.SemaphoreType.DMA((4,)),
            pltpu.SemaphoreType.DMA,
            pltpu.SemaphoreType.DMA,
        ],
        compiler_params=pltpu.CompilerParams(
            collective_id=0, has_side_effects=True, vmem_limit_bytes=limit
        ),
    )(*[
        pltpu.with_memory_space_constraint(argument, pltpu.HBM)
        for argument in (jnp.transpose(cache, (1, 0, 2)), lengths, slots, query)
    ])


def solution(mesh):
    return jax.shard_map(
        shards,
        mesh=mesh,
        in_specs=(
            P("grp", ("wide", "narrow"), None),
            P("grp"),
            P("grp"),
            P(("grp", "wide"), None, "narrow", None),
        ),
        out_specs=P(("grp", "wide"), None, "narrow", None),
        check_vma=False,
    )
```

profile of v0, /device:TPU:0, one launch (start us, length us, event | category | flops | bytes accessed | tf_op | source)
XLA Modules:
  0.0 9.6 jit_solution(5138552379493232077)
XLA Ops:
  0.0 9.0 %shard_map.46 = bf16[1,1,32,512]{3,2,1,0:T(8,128)(2,1)S(1)} custom-call(bf16[3,8,576]{2,1,0:T(8,128)(2,1)} %bitcast.1, s32[8]{0:T(128)} %lengths_hbm.1, s32[8]{0:T(128)} %slots_hbm.1, bf16[1,1,32,576]{3,2,1,0:T(8,128)(2,1)} %query_hbm.1), custom_call_target="tpu_custom_call" | custom-call | tf_op jit(solution)/shard_map/pallas_call | solution.py:155
  9.0 0.6 %copy.6 = bf16[1,1,32,512]{3,2,1,0:T(8,128)(2,1)} copy(bf16[1,1,32,512]{3,2,1,0:T(8,128)(2,1)S(1)} %shard_map.46) | data formatting | bytes 65536
where the time goes:
time: 9.76 us; the launch traced here: 9.59 us
  Pallas kernels  8.96 us (92%)
  local copies, waits for them, and re-layouts  0.62 us (6%)
    pallas_call x1, Pallas kernels, shards(): pl.pallas_call(functools.partial(kernel, wide_count, narrow_count), out_s...  8.96 us
    unnamed x1, local copies, waits for them, and re-layouts  0.62 us

commit v1 on v0

--- a/solution.py
+++ b/solution.py
@@ -57,7 +57,7 @@
     query_copy.start()
 
     def peer(step):
-        target = lax.rem(me + step + 1, peer_count)
+        target = step + (step >= me).astype(jnp.int32)
         return lax.div(target, narrow_count), lax.rem(target, narrow_count)
 
     barrier = pltpu.get_barrier_semaphore()

time: 9.76 us -> 9.75 us (level)
  no operation moved by 1% of the time
where the time goes in v1:
time: 9.75 us; the launch traced here: 9.59 us
  Pallas kernels  8.96 us (92%)
  local copies, waits for them, and re-layouts  0.62 us (6%)
    pallas_call x1, Pallas kernels, shards(): pl.pallas_call(functools.partial(kernel, wide_count, narrow_count), out_s...  8.96 us
    unnamed x1, local copies, waits for them, and re-layouts  0.62 us

profile of v1, /device:TPU:0, one launch (start us, length us, event | category | flops | bytes accessed | tf_op | source)
XLA Modules:
  0.0 9.6 jit_solution(209064092926078952)
XLA Ops:
  0.0 9.0 %shard_map.46 = bf16[1,1,32,512]{3,2,1,0:T(8,128)(2,1)S(1)} custom-call(bf16[3,8,576]{2,1,0:T(8,128)(2,1)} %bitcast.1, s32[8]{0:T(128)} %lengths_hbm.1, s32[8]{0:T(128)} %slots_hbm.1, bf16[1,1,32,576]{3,2,1,0:T(8,128)(2,1)} %query_hbm.1), custom_call_target="tpu_custom_call" | custom-call | tf_op jit(solution)/shard_map/pallas_call | solution.py:155
  9.0 0.6 %copy.6 = bf16[1,1,32,512]{3,2,1,0:T(8,128)(2,1)} copy(bf16[1,1,32,512]{3,2,1,0:T(8,128)(2,1)S(1)} %shard_map.46) | data formatting | bytes 65536

commit v2 on v0

--- a/solution.py
+++ b/solution.py
@@ -84,7 +84,6 @@
         term = jnp.dot(pick, cache_ref[offset], preferred_element_type=jnp.float32)
         ordered = term if ordered is None else ordered + term
     outgoing[...] = ordered.reshape(outgoing.shape).astype(jnp.bfloat16)
-    received[me] = outgoing[wide_index]
     pl.semaphore_wait(barrier, peer_count - 1)
 
     def send(step):
@@ -99,6 +98,7 @@
         ).start()
 
     loop(peer_count - 1, send)
+    received[me] = outgoing[wide_index]
     lengths_copy.wait()
     query_copy.wait()
     own_length = jnp.sum(

time: 9.76 us -> 9.76 us (level)
  no operation moved by 1% of the time
where the time goes in v2:
time: 9.76 us; the launch traced here: 9.59 us
  Pallas kernels  8.97 us (92%)
  local copies, waits for them, and re-layouts  0.62 us (6%)
    pallas_call x1, Pallas kernels, shards(): pl.pallas_call(functools.partial(kernel, wide_count, narrow_count), out_s...  8.97 us
    unnamed x1, local copies, waits for them, and re-layouts  0.62 us

profile of v2, /device:TPU:0, one launch (start us, length us, event | category | flops | bytes accessed | tf_op | source)
XLA Modules:
  0.0 9.6 jit_solution(1372302813833641040)
XLA Ops:
  0.0 9.0 %shard_map.46 = bf16[1,1,32,512]{3,2,1,0:T(8,128)(2,1)S(1)} custom-call(bf16[3,8,576]{2,1,0:T(8,128)(2,1)} %bitcast.1, s32[8]{0:T(128)} %lengths_hbm.1, s32[8]{0:T(128)} %slots_hbm.1, bf16[1,1,32,576]{3,2,1,0:T(8,128)(2,1)} %query_hbm.1), custom_call_target="tpu_custom_call" | custom-call | tf_op jit(solution)/shard_map/pallas_call | solution.py:155
  9.0 0.6 %copy.6 = bf16[1,1,32,512]{3,2,1,0:T(8,128)(2,1)} copy(bf16[1,1,32,512]{3,2,1,0:T(8,128)(2,1)S(1)} %shard_map.46) | data formatting | bytes 65536
